TPU v7x, 32 devices: a whole 2x2x4 slice. The times are simulated.
32 devices in a mesh: band: 2 (over x), row: 16 (over z, y, core).
Axes of the slice: x: 2, y: 2, z: 4, core: 2. Of those that a mesh axis runs over, the one named last changes fastest.
Arguments:
- shot_traces: bfloat16 [16384, 4096], P(('band', 'row')), parts along dimension 0, may hold values from -6 to 6
- source_cell: int32 [16384], P(('band', 'row')), parts along dimension 0, may hold values from 0 to 127
- receiver_cell: int32 [16384], P(('band', 'row')), parts along dimension 0, may hold values from 0 to 127
- band_order: int32 [64], P('band'), parts along dimension 0, may hold values from 0 to 31, each once
Outputs:
- next_grid: float32 [64, 2, 128, 128], P(('band', 'row')), parts along dimension 0
There are 2 independent parts, one for each index of `band`. A program takes and returns all parts, laid end to end along the dimension named above; each array names one. Nothing has to cross between parts.
Inputs may be any that keep to these rules, and one draw needn't show every extreme that they name: `band_order`: a permutation of 0 to 31.
All inputs are finite; a program needn't handle non-finite values.
Results may differ from a plain program's by a relative error of at most 0.0037.
Values may be sent and summed in bfloat16 or wider, within the bound.
A program may use at most 64 MiB of HBM per device.

v0:
```python
import functools
import math

import jax
import jax.numpy as jnp
import ml_dtypes
import numpy as np
from jax import lax
from jax.experimental import pallas as pl
from jax.experimental.pallas import tpu as pltpu
from jax.sharding import PartitionSpec as P

FLO = 64
SC = 128
RC = 128
PIECES = 4
GROUP = 4
BF = jnp.bfloat16
F32 = jnp.float32
NT_DIMS = (((1,), (1,)), ((), ()))
TN_DIMS = (((0,), (0,)), ((), ()))


def natural_table(samples_count, band_size):
    bins = FLO + np.arange(band_size)
    phase = (bins[:, None] * np.arange(samples_count)[None, :]) % samples_count
    angle = 2.0 * math.pi * phase / samples_count
    scale = 1.0 / math.sqrt(samples_count)
    table = np.stack([np.cos(angle) * scale, -np.sin(angle) * scale], axis=1)
    return table.reshape(2 * band_size, samples_count).astype(np.float32).astype(ml_dtypes.bfloat16)


def kernel(
    n,
    traces_hbm,
    source_hbm,
    receiver_hbm,
    order_hbm,
    table_hbm,
    out_ref,
    traces,
    source,
    receiver,
    order,
    table,
    lhs,
    cells_out,
    cells_in,
    send,
    recv,
    stack,
    load_sem,
    traces_sem,
    cell_send_sem,
    cell_recv_sem,
    send_sem,
    recv_sem,
    own_sem,
):
    me = lax.axis_index("row")
    piece = traces.shape[2]
    per_device = traces.shape[1]
    rows, samples_count = table.shape
    channels = send.shape[1]

    def load(at, src, dst):
        return pltpu.make_async_copy(src, dst, load_sem.at[at])

    loads = [
        load(0, source_hbm, source),
        load(1, receiver_hbm, receiver),
        load(2, order_hbm, order),
        load(3, table_hbm, table),
    ]
    for copy in loads:
        copy.start()
    trace_loads = [
        pltpu.make_async_copy(
            traces_hbm.at[:, pl.ds(c * piece, piece)], traces.at[c], traces_sem.at[c]
        )
        for c in range(PIECES)
    ]
    for copy in trace_loads:
        copy.start()

    barrier = pltpu.get_barrier_semaphore()

    def greet(i, carry):
        pl.semaphore_signal(barrier, inc=1, device_id={"row": lax.rem(me + i, n)})
        return carry

    lax.fori_loop(1, n, greet, 0)

    loads[0].wait()
    loads[1].wait()
    cells_out[...] = source[...] * RC + receiver[...]

    loads[2].wait()
    band_size = rows // 2
    spread = (
        lax.broadcasted_iota(jnp.int32, (band_size, rows), 0)
        == lax.broadcasted_iota(jnp.int32, (band_size, rows), 1) // 2
    ).astype(BF)
    bins = jnp.broadcast_to(order[...].astype(F32), (8, band_size)).astype(BF)
    wanted = jnp.dot(bins, spread, preferred_element_type=F32)[0:1]
    part = lax.broadcasted_iota(jnp.int32, (1, rows), 1) % 2
    wanted = 2.0 * wanted + part.astype(F32)
    held = lax.broadcasted_iota(jnp.int32, (rows, rows), 0).astype(F32)
    pick = (held == wanted).astype(F32).astype(BF)
    loads[3].wait()
    for at in range(0, samples_count, 1024):
        cut = pl.ds(at, 1024)
        lhs[:, cut] = lax.dot_general(
            pick, table[:, cut], TN_DIMS, preferred_element_type=F32
        ).astype(BF)

    def cell_copy(peer, slot):
        return pltpu.make_async_remote_copy(
            src_ref=cells_out,
            dst_ref=cells_in.at[slot],
            send_sem=cell_send_sem.at[peer],
            recv_sem=cell_recv_sem.at[slot],
            device_id={"row": peer},
        )

    def value_copy(peer, slot):
        return pltpu.make_async_remote_copy(
            src_ref=send.at[peer],
            dst_ref=recv.at[slot],
            send_sem=send_sem.at[peer],
            recv_sem=recv_sem.at[slot],
            device_id={"row": peer},
        )

    spectra = jnp.zeros((rows, per_device), F32)
    for c in range(PIECES):
        if c == PIECES - 1:
            pl.semaphore_wait(barrier, n - 1)

            def send_cells(i, carry):
                cell_copy(lax.rem(me + i, n), me).start()
                return carry

            lax.fori_loop(1, n, send_cells, 0)
            own_cells = pltpu.make_async_copy(cells_out, cells_in.at[me], own_sem.at[0])
            own_cells.start()
        trace_loads[c].wait()
        spectra += lax.dot_general(
            lhs[:, c * piece : (c + 1) * piece],
            traces[c],
            NT_DIMS,
            preferred_element_type=F32,
        )
    send[...] = spectra.reshape(n, channels, per_device).astype(BF)

    def send_values(i, carry):
        value_copy(lax.rem(me + i, n), me).start()
        return carry

    lax.fori_loop(1, n, send_values, 0)
    own_values = pltpu.make_async_copy(send.at[me], recv.at[me], own_sem.at[1])
    own_values.start()

    cell_at = lax.broadcasted_iota(jnp.int32, (SC, per_device), 0).astype(F32).astype(BF)
    one = jnp.ones((SC, per_device), BF)
    none = jnp.zeros((SC, per_device), BF)
    stack[...] = jnp.zeros_like(stack)

    def add(sources):
        r_parts, w_parts = [], []
        for src in sources:
            cell = cells_in[src]
            r_parts.append(jnp.where(cell_at == (cell % RC).astype(F32).astype(BF), one, none))
            s_hot = jnp.where(cell_at == (cell // RC).astype(F32).astype(BF), one, none)
            values = recv[src]
            w_parts.append(
                jnp.concatenate(
                    [s_hot * values[m : m + 1, :] for m in range(channels)] + [s_hot],
                    axis=0,
                )
            )
        stack[...] += lax.dot_general(
            jnp.concatenate(w_parts, axis=1),
            jnp.concatenate(r_parts, axis=1),
            NT_DIMS,
            preferred_element_type=F32,
        )

    own_cells.wait()
    own_values.wait()

    def add_step(g, carry):
        sources = [g * GROUP + k for k in range(GROUP)]
        for src in sources:

            @pl.when(src != me)
            def _():
                cell_copy(src, src).wait_recv()
                value_copy(src, src).wait_recv()

        add(sources)
        return carry

    lax.fori_loop(0, n // GROUP, add_step, 0)

    scale = 1.0 / jnp.maximum(stack[channels * SC :], 1.0)
    for m in range(channels):
        out_ref[m // 2, m % 2] = stack[m * SC : (m + 1) * SC] * scale

    def drain(i, carry):
        peer = lax.rem(me + i, n)
        cell_copy(peer, me).wait_send()
        value_copy(peer, me).wait_send()
        return carry

    lax.fori_loop(1, n, drain, 0)


def local(n, shot_traces, source_cell, receiver_cell, band_order):
    local_traces, samples_count = shot_traces.shape
    band_size = band_order.shape[0]
    own_slots = band_size // n
    rows = 2 * band_size
    channels = 2 * own_slots
    piece = samples_count // PIECES
    table = jnp.asarray(natural_table(samples_count, band_size))
    anywhere = pl.BlockSpec(memory_space=pltpu.HBM)
    return pl.pallas_call(
        functools.partial(kernel, n),
        out_shape=pltpu.VMEM((own_slots, 2, SC, RC), F32),
        in_specs=[anywhere] * 5,
        out_specs=pl.BlockSpec(memory_space=pltpu.VMEM),
        scratch_shapes=[
            pltpu.VMEM((PIECES, local_traces, piece), BF),
            pltpu.VMEM((1, local_traces), jnp.int32),
            pltpu.VMEM((1, local_traces), jnp.int32),
            pltpu.VMEM((1, band_size), jnp.int32),
            pltpu.VMEM((rows, samples_count), BF),
            pltpu.VMEM((rows, samples_count), BF),
            pltpu.VMEM((1, local_traces), jnp.int32),
            pltpu.VMEM((n, 1, local_traces), jnp.int32),
            pltpu.VMEM((n, channels, local_traces), BF),
            pltpu.VMEM((n, channels, local_traces), BF),
            pltpu.VMEM(((channels + 1) * SC, RC), F32),
            pltpu.SemaphoreType.DMA((4,)),
            pltpu.SemaphoreType.DMA((PIECES,)),
            pltpu.SemaphoreType.DMA((n,)),
            pltpu.SemaphoreType.DMA((n,)),
            pltpu.SemaphoreType.DMA((n,)),
            pltpu.SemaphoreType.DMA((n,)),
            pltpu.SemaphoreType.DMA((2,)),
        ],
        compiler_params=pltpu.CompilerParams(
            collective_id=0, has_side_effects=True, vmem_limit_bytes=64 * 1024 * 1024 - 65536 - 1024 * 1024
        ),
    )(
        shot_traces,
        source_cell.reshape(1, local_traces),
        receiver_cell.reshape(1, local_traces),
        band_order.reshape(1, band_size),
        table,
    )


def solution(mesh):
    placed = (P(("band", "row"), None), P(("band", "row")), P(("band", "row")), P("band"))
    return jax.shard_map(
        functools.partial(local, mesh.shape["row"]),
        mesh=mesh,
        in_specs=placed,
        out_specs=P(("band", "row"), None, None, None),
        check_vma=False,
    )
```

profile of v0, /device:TPU:0, one launch (start us, length us, event | category | flops | bytes accessed | tf_op | source)
XLA Modules:
  0.0 14.1 jit_solution(5207246016653798127)
XLA Ops:
  0.0 13.4 %shard_map.55 = f32[2,2,128,128]{3,2,1,0:T(8,128)S(1)} custom-call(bf16[512,4096]{1,0:T(8,128)(2,1)} %traces_hbm.1, s32[1,512]{1,0:T(1,128)} %bitcast.3, s32[1,512]{1,0:T(1,128)} %bitcast.4, s32[1,32]{1,0:T(1,128)} %bitcast.5, bf16[64,4096]{1,0:T(8,128)(2,1)} %constant.2.clone.table_hbm), custom_call_target="tpu_custom_call" | custom-call | tf_op jit(solution)/shard_map/pallas_call | solution.py:228
  13.4 0.7 %copy.7 = f32[2,2,128,128]{3,2,1,0:T(8,128)} copy(f32[2,2,128,128]{3,2,1,0:T(8,128)S(1)} %shard_map.55) | data formatting | bytes 524288
where the time goes:
time: 14.2 us; the launch traced here: 14.1 us
  Pallas kernels  13.4 us (94%)
  local copies, waits for them, and re-layouts  0.71 us (5%)
    pallas_call x1, Pallas kernels, local(): pl.pallas_call(functools.partial(kernel, n), out_shape=pltpu.VMEM((own_sl...  13.4 us
    unnamed x1, local copies, waits for them, and re-layouts  0.71 us

commit v1 on v0

v1 whole, which is shorter than its diff:
```python
import functools
import math

import jax
import jax.numpy as jnp
import ml_dtypes
import numpy as np
from jax import lax
from jax.experimental import pallas as pl
from jax.experimental.pallas import tpu as pltpu
from jax.sharding import PartitionSpec as P

FLO = 64
SC = 128
RC = 128
HI = SC // 2
LO = 2 * RC
CUTS = (1024, 1024, 1024, 512, 256, 256)
PAIR = 2
BF = jnp.bfloat16
F32 = jnp.float32
NT_DIMS = (((1,), (1,)), ((), ()))


def natural_table(samples_count, band_size):
    bins = FLO + np.arange(band_size)
    phase = (bins[:, None] * np.arange(samples_count // 4)[None, :]) % samples_count
    angle = 2.0 * math.pi * phase / samples_count
    scale = 1.0 / math.sqrt(samples_count)
    table = np.stack([np.cos(angle) * scale, -np.sin(angle) * scale], axis=1)
    return table.reshape(2 * band_size, samples_count // 4).astype(np.float32).astype(ml_dtypes.bfloat16)


def pieces_of(samples_count):
    at, out = 0, []
    for part in CUTS:
        width = part * samples_count // sum(CUTS)
        out.append((at, width))
        at += width
    return out


def flip(a, b, n):
    out, bit = 0, 1
    while bit < n:
        out = out + bit * ((a // bit + b // bit) % 2)
        bit *= 2
    return out


def kernel(
    n,
    traces_hbm,
    source_hbm,
    receiver_hbm,
    order_hbm,
    table_hbm,
    out_ref,
    traces,
    source,
    receiver,
    order,
    table,
    lhs,
    cells_out,
    cells_in,
    send,
    recv,
    stack,
    load_sem,
    traces_sem,
    cell_send_sem,
    cell_recv_sem,
    send_sem,
    recv_sem,
):
    me = lax.axis_index("row")
    per_device, samples_count = traces.shape
    rows, quarter = table.shape
    band_size = rows // 2
    channels = send.shape[1]
    cuts = pieces_of(samples_count)

    loads = [
        pltpu.make_async_copy(src, dst, load_sem.at[at])
        for at, (src, dst) in enumerate(
            [(order_hbm, order), (table_hbm, table), (source_hbm, source), (receiver_hbm, receiver)]
        )
    ]
    for copy in loads:
        copy.start()
    trace_loads = [
        pltpu.make_async_copy(
            traces_hbm.at[:, pl.ds(at, width)], traces.at[:, pl.ds(at, width)], traces_sem.at[c]
        )
        for c, (at, width) in enumerate(cuts)
    ]
    for copy in trace_loads:
        copy.start()

    barrier = pltpu.get_barrier_semaphore()

    def other(k):
        return k + (k - me + n) // n

    for k in range(n - 1):
        pl.semaphore_signal(barrier, inc=1, device_id={"row": other(k)})

    stack[...] = jnp.zeros_like(stack)

    loads[0].wait()
    row_at = lax.broadcasted_iota(jnp.int32, (rows, rows), 0)
    slot_at = row_at // 2
    part = row_at % 2
    blocks = []
    for base in range(0, band_size, 4):
        at = lax.broadcasted_iota(jnp.int32, (8, rows), 0) // 2
        block = jnp.full((8, rows), order[0, base], jnp.int32)
        for k in range(1, 4):
            block = jnp.where(at == k, order[0, base + k], block)
        blocks.append(block)
    wanted = jnp.concatenate(blocks, axis=0)
    col = lax.broadcasted_iota(jnp.int32, (rows, rows), 1)
    bin_at = FLO + wanted
    same = (col == 2 * wanted + part).astype(F32)
    crossed = (col == 2 * wanted + 1 - part).astype(F32)
    picks = []
    for j in range(4):
        turn = (j * bin_at) % 4
        flat_sign = jnp.where(turn == 0, 1.0, jnp.where(turn == 2, -1.0, 0.0))
        cross_sign = jnp.where(turn % 2 == 0, 0.0, jnp.where((turn == 1) == (part == 0), 1.0, -1.0))
        picks.append((same * flat_sign + crossed * cross_sign).astype(BF))
    loads[1].wait()
    for j in range(4):
        lhs[:, j * quarter : (j + 1) * quarter] = jnp.dot(
            picks[j], table[...], preferred_element_type=F32
        ).astype(BF)

    loads[2].wait()
    loads[3].wait()
    hi = source[...] % HI
    lo = (source[...] // HI) * RC + receiver[...]
    cells_out[...] = jnp.concatenate([hi, lo], axis=0).astype(F32).astype(BF)

    def cell_copy(peer, slot):
        return pltpu.make_async_remote_copy(
            src_ref=cells_out,
            dst_ref=cells_in.at[slot],
            send_sem=cell_send_sem.at[peer],
            recv_sem=cell_recv_sem.at[slot],
            device_id={"row": peer},
        )

    def value_copy(peer, slot):
        return pltpu.make_async_remote_copy(
            src_ref=send.at[peer],
            dst_ref=recv.at[slot],
            send_sem=send_sem.at[peer],
            recv_sem=recv_sem.at[slot],
            device_id={"row": peer},
        )

    spectra = jnp.zeros((rows, per_device), F32)
    for c, (at, width) in enumerate(cuts):
        if c == len(cuts) - 2:
            pl.semaphore_wait(barrier, n - 1)
            for k in range(n - 1):
                cell_copy(other(k), me).start()
        trace_loads[c].wait()
        spectra += lax.dot_general(
            lhs[:, at : at + width], traces[:, at : at + width], NT_DIMS, preferred_element_type=F32
        )
    send[...] = spectra.reshape(n, channels, per_device).astype(BF)
    for k in range(n - 1):
        value_copy(other(k), me).start()

    lo_at = lax.broadcasted_iota(jnp.int32, (LO, per_device), 0).astype(F32).astype(BF)
    hi_at = lax.broadcasted_iota(jnp.int32, (HI, per_device), 0).astype(F32).astype(BF)
    zero = jnp.zeros((), BF)
    one = jnp.ones((), BF)

    def product(entries):
        r_parts, w_parts = [], []
        for cells, values in entries:
            r_parts.append(jnp.where(lo_at == cells[1:2, :], one, zero))
            s_hot = jnp.where(hi_at == cells[0:1, :], one, zero)
            w_parts.append(
                jnp.concatenate([s_hot * values[m : m + 1, :] for m in range(channels)] + [s_hot], axis=0)
            )
        return lax.dot_general(
            jnp.concatenate(w_parts, axis=1),
            jnp.concatenate(r_parts, axis=1),
            NT_DIMS,
            preferred_element_type=F32,
        )

    def arrived(src):
        cell_copy(src, src).wait_recv()
        value_copy(src, src).wait_recv()
        return cells_in[src], recv[src]

    partner = flip(me, 1, n)
    stack[...] = product([(cells_out[...], send[me])])
    stack[...] += product([arrived(partner)])

    def step(g, carry):
        sources = [flip(me, PAIR * g + k, n) for k in range(PAIR)]
        stack[...] += product([arrived(src) for src in sources])
        return carry

    lax.fori_loop(1, n // PAIR - 1, step, 0)

    for k in range(n - 1):
        peer = other(k)
        cell_copy(peer, me).wait_send()
        value_copy(peer, me).wait_send()

    total = stack[...] + product([arrived(flip(me, n - PAIR + k, n)) for k in range(PAIR)])
    scale = 1.0 / jnp.maximum(total[channels * HI :], 1.0)
    for m in range(channels):
        grid = total[m * HI : (m + 1) * HI] * scale
        out_ref[m // 2, m % 2, 0:HI] = grid[:, 0:RC]
        out_ref[m // 2, m % 2, HI:SC] = grid[:, RC:LO]


def local(n, shot_traces, source_cell, receiver_cell, band_order):
    local_traces, samples_count = shot_traces.shape
    band_size = band_order.shape[0]
    own_slots = band_size // n
    rows = 2 * band_size
    channels = 2 * own_slots
    table = jnp.asarray(natural_table(samples_count, band_size))
    anywhere = pl.BlockSpec(memory_space=pltpu.HBM)
    return pl.pallas_call(
        functools.partial(kernel, n),
        out_shape=pltpu.VMEM((own_slots, 2, SC, RC), F32),
        in_specs=[anywhere] * 5,
        out_specs=pl.BlockSpec(memory_space=pltpu.VMEM),
        scratch_shapes=[
            pltpu.VMEM((local_traces, samples_count), BF),
            pltpu.VMEM((1, local_traces), jnp.int32),
            pltpu.VMEM((1, local_traces), jnp.int32),
            pltpu.SMEM((1, band_size), jnp.int32),
            pltpu.VMEM((rows, samples_count // 4), BF),
            pltpu.VMEM((rows, samples_count), BF),
            pltpu.VMEM((2, local_traces), BF),
            pltpu.VMEM((n, 2, local_traces), BF),
            pltpu.VMEM((n, channels, local_traces), BF),
            pltpu.VMEM((n, channels, local_traces), BF),
            pltpu.VMEM(((channels + 1) * HI, LO), F32),
            pltpu.SemaphoreType.DMA((4,)),
            pltpu.SemaphoreType.DMA((len(CUTS),)),
            pltpu.SemaphoreType.DMA((n,)),
            pltpu.SemaphoreType.DMA((n,)),
            pltpu.SemaphoreType.DMA((n,)),
            pltpu.SemaphoreType.DMA((n,)),
        ],
        compiler_params=pltpu.CompilerParams(
            collective_id=0, has_side_effects=True, vmem_limit_bytes=64 * 1024 * 1024 - 65536 - 1024 * 1024
        ),
    )(
        shot_traces,
        source_cell.reshape(1, local_traces),
        receiver_cell.reshape(1, local_traces),
        band_order.reshape(1, band_size),
        table,
    )


def solution(mesh):
    placed = (P(("band", "row"), None), P(("band", "row")), P(("band", "row")), P("band"))
    return jax.shard_map(
        functools.partial(local, mesh.shape["row"]),
        mesh=mesh,
        in_specs=placed,
        out_specs=P(("band", "row"), None, None, None),
        check_vma=False,
    )
```

time: 14.2 us -> 13.3 us (0.937)
  Pallas kernels: 13.4 us -> 12.4 us
    pallas_call x1, Pallas kernels: 13.4 us -> 12.4 us  [local(): pl.pallas_call(functools.partial(kernel, n), out_shape=pltpu.VMEM((own_sl...]
where the time goes in v1:
time: 13.3 us; the launch traced here: 13.2 us
  Pallas kernels  12.4 us (93%)
  local copies, waits for them, and re-layouts  0.71 us (5%)
    pallas_call x1, Pallas kernels, local(): pl.pallas_call(functools.partial(kernel, n), out_shape=pltpu.VMEM((own_sl...  12.4 us
    unnamed x1, local copies, waits for them, and re-layouts  0.71 us

profile of v1, /device:TPU:0, one launch (start us, length us, event | category | flops | bytes accessed | tf_op | source)
XLA Modules:
  0.0 13.2 jit_solution(4650439418294045484)
XLA Ops:
  0.0 12.4 %shard_map.55 = f32[2,2,128,128]{3,2,1,0:T(8,128)S(1)} custom-call(bf16[512,4096]{1,0:T(8,128)(2,1)} %traces_hbm.1, s32[1,512]{1,0:T(1,128)} %bitcast.3, s32[1,512]{1,0:T(1,128)} %bitcast.4, s32[1,32]{1,0:T(1,128)} %bitcast.5, bf16[64,1024]{1,0:T(8,128)(2,1)} %constant.2.clone.table_hbm), custom_call_target="tpu_custom_call" | custom-call | tf_op jit(solution)/shard_map/pallas_call | solution.py:234
  12.5 0.7 %copy.7 = f32[2,2,128,128]{3,2,1,0:T(8,128)} copy(f32[2,2,128,128]{3,2,1,0:T(8,128)S(1)} %shard_map.55) | data formatting | bytes 524288
